TPU v7x, 16 devices: a whole 2x2x2 slice. The times are simulated.
16 devices in a mesh: stage: 2 (over z), tp: 8 (over y, x, core).
Axes of the slice: x: 2, y: 2, z: 2, core: 2. Of those that a mesh axis runs over, the one named last changes fastest.
Arguments:
- x: bfloat16 [2, 2048, 4096], P(None, 'tp')
- g: bfloat16 [2, 2, 4096], P('stage')
- w1: bfloat16 [2, 2, 4096, 14336], P('stage', None, None, 'tp')
- w2: bfloat16 [2, 2, 14336, 4096], P('stage', None, 'tp')
Outputs:
- output: bfloat16 [2, 2, 2048, 4096], P('stage', None, 'tp')
All inputs are finite; a program needn't handle non-finite values.
Results may differ from a plain program's by a relative error of at most 0.0164811.
Values are sent between devices in bfloat16 or wider.
A program may use at most 1 GiB of HBM per device.

v0:
```python
import jax
import jax.numpy as jnp
from jax import lax
from jax.sharding import PartitionSpec as P

EPS = 1e-5


def _ln(y, g):
    yf = y.astype(jnp.float32)
    mu = jnp.mean(yf, axis=-1, keepdims=True)
    var = jnp.mean(jnp.square(yf - mu), axis=-1, keepdims=True)
    return ((yf - mu) * lax.rsqrt(var + EPS) * g.astype(jnp.float32)).astype(jnp.bfloat16)


def _block(y, g, w1, w2):
    h = lax.all_gather(_ln(y, g), 'tp', axis=0, tiled=True)
    a = jax.nn.gelu(jnp.dot(h, w1, preferred_element_type=jnp.float32)).astype(jnp.bfloat16)
    p = jnp.dot(a, w2, preferred_element_type=jnp.float32).astype(jnp.bfloat16)
    r = lax.psum_scatter(p, 'tp', scatter_dimension=0, tiled=True)
    return (y.astype(jnp.float32) + r.astype(jnp.float32)).astype(jnp.bfloat16)


def solution(mesh):
    S = mesh.shape['stage']
    fwd = [(i, i + 1) for i in range(S - 1)]

    def local(x, g, w1, w2):
        s = lax.axis_index('stage')
        M = x.shape[0]
        nb = g.shape[1]
        out = jnp.zeros_like(x)
        recv = jnp.zeros_like(x[0])
        for k in range(M + S - 1):
            y = jnp.where(s == 0, x[min(k, M - 1)], recv)
            for b in range(nb):
                y = _block(y, g[0, b], w1[0, b], w2[0, b])
            m = k - s
            mc = jnp.clip(m, 0, M - 1)
            old = lax.dynamic_index_in_dim(out, mc, 0, keepdims=False)
            out = lax.dynamic_update_index_in_dim(out, jnp.where((m >= 0) & (m < M), y, old), mc, 0)
            if k < M + S - 2:
                recv = lax.ppermute(y, 'stage', fwd)
        return out[None]

    return jax.shard_map(
        local, mesh=mesh,
        in_specs=(P(None, 'tp', None), P('stage', None, None),
                  P('stage', None, None, 'tp'), P('stage', None, 'tp', None)),
        out_specs=P('stage', None, 'tp', None), check_vma=False)
```

profile of v0, /device:TPU:8, one launch (start us, length us, event | category | flops | bytes accessed | tf_op | source)
XLA Modules:
  0.0 1799.9 jit_solution(11937576710265875651)
XLA Ops:
  12.4 3.9 fusion.121
  16.4 87.0 %all-gather.7.cloned.1.call-done = bf16[2048,4096]{1,0:T(8,128)(2,1)} async-done(((bf16[256,4096]{1,0:T(8,128)(2,1)}), bf16[2048,4096]{1,0:T(8,128)(2,1)}) %all-gather.7.cloned.1.call-update) | async-done | bytes 16777232 | tf_op jit(solution)/shard_map/all_gather | solution.py:17
  103.4 39.3 %fusion.7 = bf16[2048,1792]{1,0:T(8,128)(2,1)S(1)} fusion(bf16[2048,4096]{1,0:T(8,128)(2,1)} %all-gather.7.cloned.1.call-done, bf16[1,2,4096,1792]{3,2,1,0:T(8,128)(2,1)} %param.6), kind=kOutput, calls=%fused_computation.19 | convolution fusion | flops 30097801216 | bytes 38797312 | tf_op jit(solution)/shard_map/dot_general | solution.py:18
  142.7 36.3 %convolution_convert_fusion.5 = bf16[2048,4096]{1,0:T(8,128)(2,1)} fusion(bf16[2048,1792]{1,0:T(8,128)(2,1)S(1)} %fusion.7, bf16[1,2,1792,4096]{3,2,1,0:T(8,128)(2,1)} %param.7), kind=kOutput, calls=%fused_computation.11 | convolution fusion | flops 30073159680 | bytes 38797312 | tf_op jit(solution)/shard_map/dot_general | solution.py:19
  179.1 109.8 %reduce-scatter.7.cloned.1.call-done = bf16[256,4096]{1,0:T(8,128)(2,1)} async-done(((bf16[2048,4096]{1,0:T(8,128)(2,1)}), bf16[256,4096]{1,0:T(8,128)(2,1)}) %reduce-scatter.7.cloned.1.call-update) | async-done | bytes 2097168 | tf_op jit(solution)/shard_map/reduce_scatter | solution.py:20
  288.8 3.2 convert_reduce_fusion.4
  295.0 86.0 %all-gather.9.cloned.1.call-done = bf16[2048,4096]{1,0:T(8,128)(2,1)} async-done(((bf16[256,4096]{1,0:T(8,128)(2,1)}), bf16[2048,4096]{1,0:T(8,128)(2,1)}) %all-gather.9.cloned.1.call-update) | async-done | bytes 16777232 | tf_op jit(solution)/shard_map/all_gather | solution.py:17
  381.0 40.8 %fusion.15 = bf16[2048,1792]{1,0:T(8,128)(2,1)} fusion(bf16[2048,4096]{1,0:T(8,128)(2,1)} %all-gather.9.cloned.1.call-done, bf16[1,2,4096,1792]{3,2,1,0:T(8,128)(2,1)} %param.6), kind=kOutput, calls=%fused_computation.27 | convolution fusion | flops 30097801216 | bytes 38797312 | tf_op jit(solution)/shard_map/dot_general | solution.py:18
  421.8 37.9 %convolution_convert_fusion.4 = bf16[2048,4096]{1,0:T(8,128)(2,1)} fusion(bf16[2048,1792]{1,0:T(8,128)(2,1)} %fusion.15, bf16[1,2,1792,4096]{3,2,1,0:T(8,128)(2,1)} %param.7), kind=kOutput, calls=%fused_computation.10 | convolution fusion | flops 30073159680 | bytes 38797312 | tf_op jit(solution)/shard_map/dot_general | solution.py:19
  459.7 109.8 %reduce-scatter.9.cloned.1.call-done = bf16[256,4096]{1,0:T(8,128)(2,1)} async-done(((bf16[2048,4096]{1,0:T(8,128)(2,1)}), bf16[256,4096]{1,0:T(8,128)(2,1)}) %reduce-scatter.9.cloned.1.call-update) | async-done | bytes 2097168 | tf_op jit(solution)/shard_map/reduce_scatter | solution.py:20
  574.1 47.7 %collective-permute-done = bf16[256,4096]{1,0:T(8,128)(2,1)S(1)} collective-permute-done((bf16[256,4096]{1,0:T(8,128)(2,1)S(1)}, bf16[256,4096]{1,0:T(8,128)(2,1)S(1)}, u32[]{:S(2)}, u32[]{:S(2)}) %collective-permute-start) | collective-permute-done | bytes 2097184 | tf_op jit(solution)/shard_map/ppermute | solution.py:43
  626.3 86.0 %all-gather.11.cloned.1.call-done = bf16[2048,4096]{1,0:T(8,128)(2,1)} async-done(((bf16[256,4096]{1,0:T(8,128)(2,1)}), bf16[2048,4096]{1,0:T(8,128)(2,1)}) %all-gather.11.cloned.1.call-update) | async-done | bytes 16777232 | tf_op jit(solution)/shard_map/all_gather | solution.py:17
  712.3 39.5 %fusion.23 = bf16[2048,1792]{1,0:T(8,128)(2,1)S(1)} fusion(bf16[2048,4096]{1,0:T(8,128)(2,1)} %all-gather.11.cloned.1.call-done, bf16[1,2,4096,1792]{3,2,1,0:T(8,128)(2,1)} %param.6), kind=kOutput, calls=%fused_computation.35 | convolution fusion | flops 30097801216 | bytes 38797312 | tf_op jit(solution)/shard_map/dot_general | solution.py:18
  751.7 36.1 %convolution_convert_fusion.3 = bf16[2048,4096]{1,0:T(8,128)(2,1)} fusion(bf16[2048,1792]{1,0:T(8,128)(2,1)S(1)} %fusion.23, bf16[1,2,1792,4096]{3,2,1,0:T(8,128)(2,1)} %param.7), kind=kOutput, calls=%fused_computation.9 | convolution fusion | flops 30073159680 | bytes 38797312 | tf_op jit(solution)/shard_map/dot_general | solution.py:19
  787.9 109.8 %reduce-scatter.11.cloned.1.call-done = bf16[256,4096]{1,0:T(8,128)(2,1)} async-done(((bf16[2048,4096]{1,0:T(8,128)(2,1)}), bf16[256,4096]{1,0:T(8,128)(2,1)}) %reduce-scatter.11.cloned.1.call-update) | async-done | bytes 2097168 | tf_op jit(solution)/shard_map/reduce_scatter | solution.py:20
  903.7 86.0 %all-gather.13.cloned.1.call-done = bf16[2048,4096]{1,0:T(8,128)(2,1)} async-done(((bf16[256,4096]{1,0:T(8,128)(2,1)}), bf16[2048,4096]{1,0:T(8,128)(2,1)}) %all-gather.13.cloned.1.call-update) | async-done | bytes 16777232 | tf_op jit(solution)/shard_map/all_gather | solution.py:17
  989.7 40.7 %fusion.31 = bf16[2048,1792]{1,0:T(8,128)(2,1)} fusion(bf16[2048,4096]{1,0:T(8,128)(2,1)} %all-gather.13.cloned.1.call-done, bf16[1,2,4096,1792]{3,2,1,0:T(8,128)(2,1)} %param.6), kind=kOutput, calls=%fused_computation.43 | convolution fusion | flops 30097801216 | bytes 38797312 | tf_op jit(solution)/shard_map/dot_general | solution.py:18
  1030.5 37.8 %convolution_convert_fusion.2 = bf16[2048,4096]{1,0:T(8,128)(2,1)} fusion(bf16[2048,1792]{1,0:T(8,128)(2,1)} %fusion.31, bf16[1,2,1792,4096]{3,2,1,0:T(8,128)(2,1)} %param.7), kind=kOutput, calls=%fused_computation.8 | convolution fusion | flops 30073159680 | bytes 38797312 | tf_op jit(solution)/shard_map/dot_general | solution.py:19
  1068.3 3.1 constant_dynamic-slice_fusion
  1071.5 106.6 %reduce-scatter.13.cloned.1.call-done = bf16[256,4096]{1,0:T(8,128)(2,1)} async-done(((bf16[2048,4096]{1,0:T(8,128)(2,1)}), bf16[256,4096]{1,0:T(8,128)(2,1)}) %reduce-scatter.13.cloned.1.call-update) | async-done | bytes 2097168 | tf_op jit(solution)/shard_map/reduce_scatter | solution.py:20
  1178.1 4.8 bitcast_dynamic-update-slice_fusion
  1184.2 47.7 %collective-permute-done.1 = bf16[256,4096]{1,0:T(8,128)(2,1)S(1)} collective-permute-done((bf16[256,4096]{1,0:T(8,128)(2,1)S(1)}, bf16[256,4096]{1,0:T(8,128)(2,1)S(1)}, u32[]{:S(2)}, u32[]{:S(2)}) %collective-permute-start.1) | collective-permute-done | bytes 2097184 | tf_op jit(solution)/shard_map/ppermute | solution.py:43
  1236.4 86.0 %all-gather.15.cloned.1.call-done = bf16[2048,4096]{1,0:T(8,128)(2,1)} async-done(((bf16[256,4096]{1,0:T(8,128)(2,1)}), bf16[2048,4096]{1,0:T(8,128)(2,1)}) %all-gather.15.cloned.1.call-update) | async-done | bytes 16777232 | tf_op jit(solution)/shard_map/all_gather | solution.py:17
  1322.4 39.5 %fusion.39 = bf16[2048,1792]{1,0:T(8,128)(2,1)S(1)} fusion(bf16[2048,4096]{1,0:T(8,128)(2,1)} %all-gather.15.cloned.1.call-done, bf16[1,2,4096,1792]{3,2,1,0:T(8,128)(2,1)} %param.6), kind=kOutput, calls=%fused_computation.51 | convolution fusion | flops 30097801216 | bytes 38797312 | tf_op jit(solution)/shard_map/dot_general | solution.py:18
  1361.8 36.1 %convolution_convert_fusion.1 = bf16[2048,4096]{1,0:T(8,128)(2,1)} fusion(bf16[2048,1792]{1,0:T(8,128)(2,1)S(1)} %fusion.39, bf16[1,2,1792,4096]{3,2,1,0:T(8,128)(2,1)} %param.7), kind=kOutput, calls=%fused_computation.7 | convolution fusion | flops 30073159680 | bytes 38797312 | tf_op jit(solution)/shard_map/dot_general | solution.py:19
  1398.0 109.7 %reduce-scatter.15.cloned.1.call-done = bf16[256,4096]{1,0:T(8,128)(2,1)} async-done(((bf16[2048,4096]{1,0:T(8,128)(2,1)}), bf16[256,4096]{1,0:T(8,128)(2,1)}) %reduce-scatter.15.cloned.1.call-update) | async-done | bytes 2097168 | tf_op jit(solution)/shard_map/reduce_scatter | solution.py:20
  1513.8 86.0 %all-gather.17.cloned.1.call-done = bf16[2048,4096]{1,0:T(8,128)(2,1)} async-done(((bf16[256,4096]{1,0:T(8,128)(2,1)}), bf16[2048,4096]{1,0:T(8,128)(2,1)}) %all-gather.17.cloned.1.call-update) | async-done | bytes 16777232 | tf_op jit(solution)/shard_map/all_gather | solution.py:17
  1599.8 40.8 %fusion.47 = bf16[2048,1792]{1,0:T(8,128)(2,1)} fusion(bf16[2048,4096]{1,0:T(8,128)(2,1)} %all-gather.17.cloned.1.call-done, bf16[1,2,4096,1792]{3,2,1,0:T(8,128)(2,1)} %param.6), kind=kOutput, calls=%fused_computation.59 | convolution fusion | flops 30097801216 | bytes 38797312 | tf_op jit(solution)/shard_map/dot_general | solution.py:18
  1640.5 37.6 %convolution_convert_fusion = bf16[2048,4096]{1,0:T(8,128)(2,1)} fusion(bf16[2048,1792]{1,0:T(8,128)(2,1)} %fusion.47, bf16[1,2,1792,4096]{3,2,1,0:T(8,128)(2,1)} %param.7), kind=kOutput, calls=%fused_computation.6 | convolution fusion | flops 30073159680 | bytes 38797312 | tf_op jit(solution)/shard_map/dot_general | solution.py:19
  1678.2 4.7 copy.7
  1682.9 105.1 %reduce-scatter.17.cloned.1.call-done = bf16[256,4096]{1,0:T(8,128)(2,1)} async-done(((bf16[2048,4096]{1,0:T(8,128)(2,1)}), bf16[256,4096]{1,0:T(8,128)(2,1)}) %reduce-scatter.17.cloned.1.call-update) | async-done | bytes 2097168 | tf_op jit(solution)/shard_map/reduce_scatter | solution.py:20
  1788.0 4.6 fusion.130
  (79 shorter events, 35.9 us)
Async XLA Ops:
  6.5 96.8 %all-gather.7.cloned.1.call-start = ((), (), s32[]{:S(2)}) async-start(), calls=%async_computation.6 | async-start | bytes 18874368 | tf_op jit(solution)/shard_map/all_gather | solution.py:17
  11.8 0.6 copy-start.8
  11.9 280.9 %copy-start.5 = (f32[1,1,4096]{2,1,0:T(1,128)}, f32[1,1,4096]{2,1,0:T(1,128)S(1)}, u32[]{:S(2)}) copy-start(f32[1,1,4096]{2,1,0:T(1,128)S(1)} %get-tuple-element.19) | copy-start | bytes 49156
  16.4 272.5 %reduce-scatter.7.cloned.1.call-start = ((), (), s32[]{:S(2)}) async-start(), calls=%async_computation.7 | async-start | bytes 18874368 | tf_op jit(solution)/shard_map/reduce_scatter | solution.py:20
  179.0 202.0 %all-gather.9.cloned.1.call-start = ((), (), s32[]{:S(2)}) async-start(), calls=%async_computation.8 | async-start | bytes 18874368 | tf_op jit(solution)/shard_map/all_gather | solution.py:17
  294.9 274.5 %reduce-scatter.9.cloned.1.call-start = ((), (), s32[]{:S(2)}) async-start(), calls=%async_computation.9 | async-start | bytes 18874368 | tf_op jit(solution)/shard_map/reduce_scatter | solution.py:20
  459.7 252.6 %all-gather.11.cloned.1.call-start = ((), (), s32[]{:S(2)}) async-start(), calls=%async_computation.10 | async-start | bytes 18874368 | tf_op jit(solution)/shard_map/all_gather | solution.py:17
  569.5 52.4 %copy-start = (bf16[2,256,4096]{2,1,0:T(8,128)(2,1)S(1)}, bf16[2,256,4096]{2,1,0:T(8,128)(2,1)}, u32[]{:S(2)}) copy-start(bf16[2,256,4096]{2,1,0:T(8,128)(2,1)} %param.4) | copy-start | bytes 12582916
  570.0 54.1 %copy-start.9 = (f32[1,1,4096]{2,1,0:T(1,128)S(1)}, f32[1,1,4096]{2,1,0:T(1,128)}, u32[]{:S(2)}) copy-start(f32[1,1,4096]{2,1,0:T(1,128)} %copy-done.8) | copy-start | bytes 49156
  572.8 49.9 %copy-start.2 = (bf16[2,256,4096]{2,1,0:T(8,128)(2,1)}, bf16[2,256,4096]{2,1,0:T(8,128)(2,1)S(1)}, u32[]{:S(2)}) copy-start(bf16[2,256,4096]{2,1,0:T(8,128)(2,1)S(1)} %get-tuple-element.15) | copy-start | bytes 12582916
  572.8 49.0 %collective-permute-start = (bf16[256,4096]{1,0:T(8,128)(2,1)S(1)}, bf16[256,4096]{1,0:T(8,128)(2,1)S(1)}, u32[]{:S(2)}, u32[]{:S(2)}) collective-permute-start(bf16[256,4096]{1,0:T(8,128)(2,1)S(1)} %get-tuple-element.16), channel_id=1, source_target_pairs={{0,8},{1,9},{2,10},{3,11},{4,12},{5,13},{6,14},{7,15}} | collective-permute-start | bytes 6291464 | tf_op jit(solution)/shard_map/ppermute | solution.py:43
  622.7 1.3 copy-start.4
  626.2 271.4 %reduce-scatter.11.cloned.1.call-start = ((), (), s32[]{:S(2)}) async-start(), calls=%async_computation.11 | async-start | bytes 18874368 | tf_op jit(solution)/shard_map/reduce_scatter | solution.py:20
  787.9 113.6 %copy-start.6 = (f32[1,1,4096]{2,1,0:T(1,128)S(1)}, f32[1,1,4096]{2,1,0:T(1,128)}, u32[]{:S(2)}) copy-start(f32[1,1,4096]{2,1,0:T(1,128)} %copy-done.5) | copy-start | bytes 49156
  787.9 201.8 %all-gather.13.cloned.1.call-start = ((), (), s32[]{:S(2)}) async-start(), calls=%async_computation.12 | async-start | bytes 18874368 | tf_op jit(solution)/shard_map/all_gather | solution.py:17
  903.7 274.4 %reduce-scatter.13.cloned.1.call-start = ((), (), s32[]{:S(2)}) async-start(), calls=%async_computation.13 | async-start | bytes 18874368 | tf_op jit(solution)/shard_map/reduce_scatter | solution.py:20
  1068.3 254.1 %all-gather.15.cloned.1.call-start = ((), (), s32[]{:S(2)}) async-start(), calls=%async_computation.14 | async-start | bytes 18874368 | tf_op jit(solution)/shard_map/all_gather | solution.py:17
  1071.5 162.7 %copy-start.10 = (f32[1,1,4096]{2,1,0:T(1,128)S(1)}, f32[1,1,4096]{2,1,0:T(1,128)}, u32[]{:S(2)}) copy-start(f32[1,1,4096]{2,1,0:T(1,128)} %copy-done.8) | copy-start | bytes 49156
  1178.1 53.9 %copy-start.1 = (bf16[2,256,4096]{2,1,0:T(8,128)(2,1)S(1)}, bf16[2,256,4096]{2,1,0:T(8,128)(2,1)}, u32[]{:S(2)}) copy-start(bf16[2,256,4096]{2,1,0:T(8,128)(2,1)} %param.4) | copy-start | bytes 12582916
  1183.0 49.0 %collective-permute-start.1 = (bf16[256,4096]{1,0:T(8,128)(2,1)S(1)}, bf16[256,4096]{1,0:T(8,128)(2,1)S(1)}, u32[]{:S(2)}, u32[]{:S(2)}) collective-permute-start(bf16[256,4096]{1,0:T(8,128)(2,1)S(1)} %get-tuple-element.10), channel_id=1, source_target_pairs={{0,8},{1,9},{2,10},{3,11},{4,12},{5,13},{6,14},{7,15}} | collective-permute-start | bytes 6291464 | tf_op jit(solution)/shard_map/ppermute | solution.py:43
  1232.8 1.3 copy-start.3
  1236.4 271.4 %reduce-scatter.15.cloned.1.call-start = ((), (), s32[]{:S(2)}) async-start(), calls=%async_computation.15 | async-start | bytes 18874368 | tf_op jit(solution)/shard_map/reduce_scatter | solution.py:20
  1398.0 113.6 %copy-start.7 = (f32[1,1,4096]{2,1,0:T(1,128)S(1)}, f32[1,1,4096]{2,1,0:T(1,128)}, u32[]{:S(2)}) copy-start(f32[1,1,4096]{2,1,0:T(1,128)} %copy-done.5) | copy-start | bytes 49156
  1398.0 201.8 %all-gather.17.cloned.1.call-start = ((), (), s32[]{:S(2)}) async-start(), calls=%async_computation.16 | async-start | bytes 18874368 | tf_op jit(solution)/shard_map/all_gather | solution.py:17
  1513.7 274.3 %reduce-scatter.17.cloned.1.call-start = ((), (), s32[]{:S(2)}) async-start(), calls=%async_computation.17 | async-start | bytes 18874368 | tf_op jit(solution)/shard_map/reduce_scatter | solution.py:20
Sparse Core Ops, SparseCore 0:
  16.5 86.8 all-gather.6
  179.1 109.6 reduce-scatter.6
  295.1 85.8 all-gather.8
  459.8 109.6 reduce-scatter.8
  626.4 85.8 all-gather.10
  788.0 109.6 reduce-scatter.10
  903.8 85.8 all-gather.12
  1068.4 109.6 reduce-scatter.12
  1236.5 85.8 all-gather.14
  1398.1 109.6 reduce-scatter.14
  1513.9 85.8 all-gather.16
  1678.3 109.6 reduce-scatter.16
where the time goes:
time: 1810 us; the launch traced here: 1800 us
  waiting for transfers between devices  1260 us (70%)
  matrix products  462 us (26%)
  other arithmetic  46.9 us (3%)
    reduce_scatter x6, waiting for transfers between devices, _block(): r = lax.psum_scatter(p, 'tp', scatter_dimension=0, tiled=True)  651 us
    all_gather x6, waiting for transfers between devices, _block(): h = lax.all_gather(_ln(y, g), 'tp', axis=0, tiled=True)  517 us
    dot_general x6, matrix products, _block(): jnp.dot(h, w1, preferred_element_type=jnp.float32)  240 us
    dot_general x6, matrix products, _block(): p = jnp.dot(a, w2, preferred_element_type=jnp.float32).astype(jnp.bfloat16)  222 us
    ppermute x2, waiting for transfers between devices, local(): recv = lax.ppermute(y, 'stage', fwd)  95.4 us
  transfers between devices with their start and end apart: 14, of which 14 were waited for; matrix products, arithmetic and copies ran while one was open for 0% of the time, Pallas kernels for 0%

commit v1 on v0

v1 whole, which is shorter than its diff:
```python
import functools

import jax
import jax.numpy as jnp
from jax import lax
from jax.experimental import pallas as pl
from jax.experimental.pallas import tpu as pltpu
from jax.sharding import PartitionSpec as P

EPS = 1e-5
BF = jnp.bfloat16
F32 = jnp.float32
MESH = pl.DeviceIdType.MESH

CHUNKS = 16
NC = 4
TN1, TN2 = 256, 512
NB = 4


def _kernel(x_ref, g_ref, w1_ref, w2_ref, out_ref, ybuf, h8, p8, r0, r1, r2, abuf, w1b, w2b,
            ssem, rsem, zs, zr, osem, xsem, w1s, w2s):
    n, c, D = x_ref.shape
    nb, _, F = w1_ref.shape
    NT1, NT2 = F // TN1, D // TN2
    U = n * nb
    stage = lax.axis_index('stage')
    tp = lax.axis_index('tp')
    py, px, co = tp // 4, (tp // 2) % 2, tp % 2
    p1 = ((py + (1 - co) * (1 - 2 * py)) * 2 + px + co * (1 - 2 * px)) * 2 + co
    p2 = ((py + co * (1 - 2 * py)) * 2 + px + (1 - co) * (1 - 2 * px)) * 2 + co
    sib = (py * 2 + px) * 2 + 1 - co

    def unit(u):
        ctx = u % NC
        return ctx, (u // (nb * NC)) * NC + ctx, (u // NC) % nb

    def remote(src, dst, i, ctx, to):
        return pltpu.make_async_remote_copy(
            src_ref=src, dst_ref=dst, send_sem=ssem.at[i, ctx], recv_sem=rsem.at[i, ctx],
            device_id=(stage, to), device_id_type=MESH)

    def rows(ref, ctx, lo, hi):
        return ref.at[ctx, pl.ds(lo * c, (hi - lo) * c)]

    def ag1(x): return remote(rows(h8, x, 0, 1), rows(h8, x, 1, 2), 0, x, p1)
    def ag2(x): return remote(rows(h8, x, 0, 2), rows(h8, x, 2, 4), 1, x, p2)
    def ag3(x): return remote(rows(h8, x, 0, 4), rows(h8, x, 4, 8), 2, x, sib)
    def rs0(x): return remote(rows(p8, x, 4, 8), r0.at[x], 3, x, sib)
    def rs1(x): return remote(rows(p8, x, 2, 4), r1.at[x], 4, x, p2)
    def rs2(x): return remote(rows(p8, x, 1, 2), r2.at[x], 5, x, p1)

    def rs0_piece(x, t):
        cols = pl.ds(pl.multiple_of(t * TN2, TN2), TN2)
        return remote(p8.at[x, pl.ds(4 * c, 4 * c), cols], r0.at[x, :, cols], 3, x, sib)

    def zcopy(k):
        return pltpu.make_async_remote_copy(
            src_ref=ybuf.at[k], dst_ref=ybuf.at[k], send_sem=zs.at[k], recv_sem=zr.at[k],
            device_id=(1 - stage, tp), device_id_type=MESH)

    def ocopy(k):
        return pltpu.make_async_copy(ybuf.at[k], out_ref.at[k], osem.at[k])

    def w1copy(i):
        cols = pl.ds(pl.multiple_of((i % NT1) * TN1, TN1), TN1)
        return pltpu.make_async_copy(w1_ref.at[(i // (NT1 * NC)) % nb, :, cols], w1b.at[i % NB], w1s.at[i % NB])

    def w2copy(i):
        cols = pl.ds(pl.multiple_of((i % NT2) * TN2, TN2), TN2)
        return pltpu.make_async_copy(w2_ref.at[(i // (NT2 * NC)) % nb, :, cols], w2b.at[i % NB], w2s.at[i % NB])

    for i in range(NB - 1):
        w1copy(i).start()
        w2copy(i).start()

    @pl.when(stage == 0)
    def _():
        cp = pltpu.make_async_copy(x_ref, ybuf, xsem)
        cp.start()
        cp.wait()

    barrier = pltpu.get_barrier_semaphore()
    for to in ((stage, p1), (stage, p2), (stage, sib), (1 - stage, tp)):
        pl.semaphore_signal(barrier, inc=1, device_id=to, device_id_type=MESH)
    pl.semaphore_wait(barrier, 4)

    def ev_a(u):
        ctx, k, b = unit(u)

        @pl.when(jnp.logical_and(stage == 1, b == 0))
        def _():
            zcopy(k).wait_recv()
        yf = ybuf[k].astype(F32)
        mu = jnp.mean(yf, axis=-1, keepdims=True)
        yc = yf - mu
        var = jnp.mean(jnp.square(yc), axis=-1, keepdims=True)
        gb = g_ref[b].astype(F32)
        h8[ctx, pl.ds(0, c), :] = (yc * lax.rsqrt(var + EPS) * gb).astype(BF)
        ag1(ctx).start()

    def ev_b(u):
        ctx = unit(u)[0]
        ag1(ctx).wait()
        ag2(ctx).start()

    def ev_c(u):
        ctx = unit(u)[0]
        ag2(ctx).wait()
        ag3(ctx).start()

    def ev_e(u):
        ctx = unit(u)[0]
        rs0(ctx).wait()
        lo = pl.ds(2 * c, 2 * c)
        p8[ctx, lo, :] = (p8[ctx, lo, :].astype(F32) + r0[ctx, lo, :].astype(F32)).astype(BF)
        rs1(ctx).start()

    def ev_f(u):
        ctx = unit(u)[0]
        rs1(ctx).wait()
        lo = pl.ds(c, c)
        p8[ctx, lo, :] = (p8[ctx, lo, :].astype(F32) + r0[ctx, lo, :].astype(F32)
                          + r1[ctx, lo, :].astype(F32)).astype(BF)
        rs2(ctx).start()

    def ev_g(u):
        ctx, k, b = unit(u)
        rs2(ctx).wait()
        lo = pl.ds(0, c)
        ybuf[k] = (ybuf[k].astype(F32)
                   + (p8[ctx, lo, :].astype(F32) + r0[ctx, lo, :].astype(F32)
                      + r1[ctx, lo, :].astype(F32) + r2[ctx].astype(F32))).astype(BF)

        @pl.when(b == nb - 1)
        def _():
            ocopy(k).start()

            @pl.when(stage == 0)
            def _():
                zcopy(k).start()

    def guarded(f, u):
        @pl.when(jnp.logical_and(u >= 0, u < U))
        def _():
            f(u)

    def round_(step, carry):
        r = step - 2
        valid = jnp.logical_and(r >= 0, r < U)

        @pl.when(valid)
        def _():
            ag3(r % NC).wait()

        def t1(t, carry):
            @pl.when(valid)
            def _():
                i = r * NT1 + t
                ctx = r % NC

                @pl.when(i + NB - 1 < U * NT1)
                def _():
                    w1copy(i + NB - 1).start()
                w1copy(i).wait()
                z = jnp.dot(h8[ctx], w1b[i % NB], preferred_element_type=F32)
                abuf[:, pl.ds(pl.multiple_of(t * TN1, TN1), TN1)] = jax.nn.gelu(z).astype(BF)

            @pl.when(t == 1)
            def _():
                guarded(ev_e, r - 1)
                guarded(ev_g, r - 2)
                guarded(ev_a, r + 2)
                guarded(ev_c, r + 1)
            return carry

        lax.fori_loop(0, NT1, t1, 0)

        def t2(t, carry):
            @pl.when(valid)
            def _():
                i = r * NT2 + t
                ctx = r % NC

                @pl.when(i + NB - 1 < U * NT2)
                def _():
                    w2copy(i + NB - 1).start()
                w2copy(i).wait()
                z = jnp.dot(abuf[...], w2b[i % NB], preferred_element_type=F32)
                p8[ctx, :, pl.ds(pl.multiple_of(t * TN2, TN2), TN2)] = z.astype(BF)

                @pl.when(t > 0)
                def _():
                    rs0_piece(ctx, t - 1).start()

            @pl.when(t == 2)
            def _():
                guarded(ev_b, r + 2)
            return carry

        lax.fori_loop(0, NT2, t2, 0)

        @pl.when(valid)
        def _():
            rs0_piece(r % NC, NT2 - 1).start()
        guarded(ev_f, r - 1)
        return carry

    lax.fori_loop(0, U + 4, round_, 0)

    def drain(k, carry):
        ocopy(k).wait()

        @pl.when(stage == 0)
        def _():
            zcopy(k).wait_send()
        return carry

    lax.fori_loop(0, n, drain, 0)


def solution(mesh):
    def local(x, g, w1, w2):
        M, T, D = x.shape
        n = CHUNKS
        c = M * T // n
        F = w1.shape[-1]
        any_ = pl.BlockSpec(memory_space=pl.ANY)
        out = pl.pallas_call(
            _kernel,
            out_shape=jax.ShapeDtypeStruct((n, c, D), BF),
            in_specs=[any_, pl.BlockSpec(memory_space=pltpu.VMEM), any_, any_],
            out_specs=any_,
            scratch_shapes=[
                pltpu.VMEM((n, c, D), BF),
                pltpu.VMEM((NC, 8 * c, D), BF),
                pltpu.VMEM((NC, 8 * c, D), BF),
                pltpu.VMEM((NC, 4 * c, D), BF),
                pltpu.VMEM((NC, 2 * c, D), BF),
                pltpu.VMEM((NC, c, D), BF),
                pltpu.VMEM((8 * c, F), BF),
                pltpu.VMEM((NB, D, TN1), BF),
                pltpu.VMEM((NB, F, TN2), BF),
                pltpu.SemaphoreType.DMA((6, NC)),
                pltpu.SemaphoreType.DMA((6, NC)),
                pltpu.SemaphoreType.DMA((n,)),
                pltpu.SemaphoreType.DMA((n,)),
                pltpu.SemaphoreType.DMA((n,)),
                pltpu.SemaphoreType.DMA,
                pltpu.SemaphoreType.DMA((NB,)),
                pltpu.SemaphoreType.DMA((NB,)),
            ],
            compiler_params=pltpu.CompilerParams(
                collective_id=0, has_side_effects=True, vmem_limit_bytes=60 * 1024 * 1024),
        )(x.reshape(n, c, D), g[0][:, None], w1[0], w2[0])
        return out.reshape(1, M, T, D)

    return jax.shard_map(
        local, mesh=mesh,
        in_specs=(P(None, 'tp', None), P('stage', None, None),
                  P('stage', None, None, 'tp'), P('stage', None, 'tp', None)),
        out_specs=P('stage', None, 'tp', None), check_vma=False)
```

time: 1810 us -> 805 us (0.44)
  waiting for transfers between devices: 1260 us -> 0 us
  Pallas kernels: 0 us -> 798 us
  matrix products: 462 us -> 0 us
  other arithmetic: 46.9 us -> 0 us
    pallas_call x0 -> x1, Pallas kernels: none -> 798 us  [local(): pl.pallas_call(_kernel, out_shape=jax.ShapeDtypeStruct((n, c, D), BF), in...]
    reduce_scatter x6 -> x0, waiting for transfers between devices: 651 us -> none  [_block(): r = lax.psum_scatter(p, 'tp', scatter_dimension=0, tiled=True)]
    all_gather x6 -> x0, waiting for transfers between devices: 517 us -> none  [_block(): h = lax.all_gather(_ln(y, g), 'tp', axis=0, tiled=True)]
    dot_general x12 -> x0, matrix products: 462 us -> none  [the longest x6 240 us: _block(): jnp.dot(h, w1, preferred_element_type=jnp.float32)]
    ppermute x2 -> x0, waiting for transfers between devices: 95.4 us -> none  [local(): recv = lax.ppermute(y, 'stage', fwd)]
    reduce_sum x12 -> x0, other arithmetic: 18.9 us -> none  [the longest x6 13 us: _ln(): mu = jnp.mean(yf, axis=-1, keepdims=True)]
  transfers between devices with their start and end apart: 14 -> 0, of which waited for: 14 -> 0; matrix products, arithmetic and copies ran while one was open for 0% -> 0% of each run, Pallas kernels for 0% -> 0%
where the time goes in v1:
time: 805 us; the launch traced here: 804 us
  Pallas kernels  798 us (99%)
    pallas_call x1, Pallas kernels, local(): pl.pallas_call(_kernel, out_shape=jax.ShapeDtypeStruct((n, c, D), BF), in...  798 us

profile of v1, /device:TPU:8, one launch (start us, length us, event | category | flops | bytes accessed | tf_op | source)
XLA Modules:
  0.0 803.6 jit_solution(13356511726500368775)
XLA Ops:
  0.0 1.4 copy.5.g_ref
  1.4 797.5 %shard_map.46 = bf16[16,32,4096]{2,1,0:T(8,128)(2,1)} custom-call(bf16[16,32,4096]{2,1,0:T(8,128)(2,1)} %bitcast.8, bf16[2,1,4096]{2,1,0:T(2,128)(2,1)} %copy.5.g_ref, bf16[2,4096,1792]{2,1,0:T(8,128)(2,1)} %bitcast.5, bf16[2,1792,4096]{2,1,0:T(8,128)(2,1)} %bitcast.6), custom_call_target="tpu_custom_call" | custom-call | tf_op jit(solution)/shard_map/pallas_call | solution.py:229
  798.9 4.7 copy.7

commit v2 on v1

--- a/solution.py
+++ b/solution.py
@@ -16,6 +16,7 @@
 NC = 4
 TN1, TN2 = 256, 512
 NB = 4
+H = 2
 
 
 def _kernel(x_ref, g_ref, w1_ref, w2_ref, out_ref, ybuf, h8, p8, r0, r1, r2, abuf, w1b, w2b,
@@ -24,6 +25,7 @@
     nb, _, F = w1_ref.shape
     NT1, NT2 = F // TN1, D // TN2
     U = n * nb
+    DH = D // H
     stage = lax.axis_index('stage')
     tp = lax.axis_index('tp')
     py, px, co = tp // 4, (tp // 2) % 2, tp % 2
@@ -40,27 +42,29 @@
             src_ref=src, dst_ref=dst, send_sem=ssem.at[i, ctx], recv_sem=rsem.at[i, ctx],
             device_id=(stage, to), device_id_type=MESH)
 
-    def rows(ref, ctx, lo, hi):
-        return ref.at[ctx, pl.ds(lo * c, (hi - lo) * c)]
-
-    def ag1(x): return remote(rows(h8, x, 0, 1), rows(h8, x, 1, 2), 0, x, p1)
-    def ag2(x): return remote(rows(h8, x, 0, 2), rows(h8, x, 2, 4), 1, x, p2)
-    def ag3(x): return remote(rows(h8, x, 0, 4), rows(h8, x, 4, 8), 2, x, sib)
-    def rs0(x): return remote(rows(p8, x, 4, 8), r0.at[x], 3, x, sib)
-    def rs1(x): return remote(rows(p8, x, 2, 4), r1.at[x], 4, x, p2)
-    def rs2(x): return remote(rows(p8, x, 1, 2), r2.at[x], 5, x, p1)
+    def part(ref, ctx, lo, hi, h):
+        return ref.at[ctx, pl.ds(lo * c, (hi - lo) * c), pl.ds(h * DH, DH)]
+
+    def ag1(x, h): return remote(part(h8, x, 0, 1, h), part(h8, x, 1, 2, h), h, x, p1)
+    def ag2(x, h): return remote(part(h8, x, 0, 2, h), part(h8, x, 2, 4, h), 2 + h, x, p2)
+    def ag3(x, h): return remote(part(h8, x, 0, 4, h), part(h8, x, 4, 8, h), 4 + h, x, sib)
+    def rs0(x, h): return remote(part(p8, x, 4, 8, h), part(r0, x, 0, 4, h), 6 + h, x, sib)
+    def rs1(x, h): return remote(part(p8, x, 2, 4, h), part(r1, x, 0, 2, h), 8 + h, x, p2)
+    def rs2(x, h): return remote(part(p8, x, 1, 2, h), part(r2, x, 0, 1, h), 10 + h, x, p1)
 
     def rs0_piece(x, t):
         cols = pl.ds(pl.multiple_of(t * TN2, TN2), TN2)
-        return remote(p8.at[x, pl.ds(4 * c, 4 * c), cols], r0.at[x, :, cols], 3, x, sib)
-
-    def zcopy(k):
+        return remote(p8.at[x, pl.ds(4 * c, 4 * c), cols], r0.at[x, :, cols], 6 + t * TN2 // DH, x, sib)
+
+    def zcopy(k, h):
+        half = ybuf.at[k, :, pl.ds(h * DH, DH)]
         return pltpu.make_async_remote_copy(
-            src_ref=ybuf.at[k], dst_ref=ybuf.at[k], send_sem=zs.at[k], recv_sem=zr.at[k],
+            src_ref=half, dst_ref=half, send_sem=zs.at[k, h], recv_sem=zr.at[k, h],
             device_id=(1 - stage, tp), device_id_type=MESH)
 
-    def ocopy(k):
-        return pltpu.make_async_copy(ybuf.at[k], out_ref.at[k], osem.at[k])
+    def ocopy(k, h):
+        cols = pl.ds(h * DH, DH)
+        return pltpu.make_async_copy(ybuf.at[k, :, cols], out_ref.at[k, :, cols], osem.at[k, h])
 
     def w1copy(i):
         cols = pl.ds(pl.multiple_of((i % NT1) * TN1, TN1), TN1)
@@ -90,60 +94,74 @@
 
         @pl.when(jnp.logical_and(stage == 1, b == 0))
         def _():
-            zcopy(k).wait_recv()
+            for h in range(H):
+                zcopy(k, h).wait_recv()
         yf = ybuf[k].astype(F32)
         mu = jnp.mean(yf, axis=-1, keepdims=True)
         yc = yf - mu
         var = jnp.mean(jnp.square(yc), axis=-1, keepdims=True)
         gb = g_ref[b].astype(F32)
         h8[ctx, pl.ds(0, c), :] = (yc * lax.rsqrt(var + EPS) * gb).astype(BF)
-        ag1(ctx).start()
-
-    def ev_b(u):
-        ctx = unit(u)[0]
-        ag1(ctx).wait()
-        ag2(ctx).start()
-
-    def ev_c(u):
-        ctx = unit(u)[0]
-        ag2(ctx).wait()
-        ag3(ctx).start()
-
-    def ev_e(u):
-        ctx = unit(u)[0]
-        rs0(ctx).wait()
-        lo = pl.ds(2 * c, 2 * c)
-        p8[ctx, lo, :] = (p8[ctx, lo, :].astype(F32) + r0[ctx, lo, :].astype(F32)).astype(BF)
-        rs1(ctx).start()
-
-    def ev_f(u):
-        ctx = unit(u)[0]
-        rs1(ctx).wait()
-        lo = pl.ds(c, c)
-        p8[ctx, lo, :] = (p8[ctx, lo, :].astype(F32) + r0[ctx, lo, :].astype(F32)
-                          + r1[ctx, lo, :].astype(F32)).astype(BF)
-        rs2(ctx).start()
-
-    def ev_g(u):
+        for h in range(H):
+            ag1(ctx, h).start()
+
+    def ev_b(u, h):
+        ctx = unit(u)[0]
+        ag1(ctx, h).wait()
+        ag2(ctx, h).start()
+
+    def ev_c(u, h):
+        ctx = unit(u)[0]
+        ag2(ctx, h).wait()
+        ag3(ctx, h).start()
+
+    def ev_e(u, h):
+        ctx = unit(u)[0]
+        rs0(ctx, h).wait()
+        at = (ctx, pl.ds(2 * c, 2 * c), pl.ds(h * DH, DH))
+        p8[at] = (p8[at].astype(F32) + r0[at].astype(F32)).astype(BF)
+        rs1(ctx, h).start()
+
+    def ev_f(u, h):
+        ctx = unit(u)[0]
+        rs1(ctx, h).wait()
+        at = (ctx, pl.ds(c, c), pl.ds(h * DH, DH))
+        p8[at] = (p8[at].astype(F32) + r0[at].astype(F32) + r1[at].astype(F32)).astype(BF)
+        rs2(ctx, h).start()
+
+    def ev_g(u, h):
         ctx, k, b = unit(u)
-        rs2(ctx).wait()
-        lo = pl.ds(0, c)
-        ybuf[k] = (ybuf[k].astype(F32)
-                   + (p8[ctx, lo, :].astype(F32) + r0[ctx, lo, :].astype(F32)
-                      + r1[ctx, lo, :].astype(F32) + r2[ctx].astype(F32))).astype(BF)
+        rs2(ctx, h).wait()
+        at = (ctx, pl.ds(0, c), pl.ds(h * DH, DH))
+        yat = (k, slice(None), pl.ds(h * DH, DH))
+        ybuf[yat] = (ybuf[yat].astype(F32)
+                     + (p8[at].astype(F32) + r0[at].astype(F32)
+                        + r1[at].astype(F32) + r2[at].astype(F32))).astype(BF)
 
         @pl.when(b == nb - 1)
         def _():
-            ocopy(k).start()
+            ocopy(k, h).start()
 
             @pl.when(stage == 0)
             def _():
-                zcopy(k).start()
-
-    def guarded(f, u):
+                zcopy(k, h).start()
+
+    def guarded(f, u, *h):
         @pl.when(jnp.logical_and(u >= 0, u < U))
         def _():
-            f(u)
+            f(u, *h)
+
+    events = ((1, ev_g, -2, 1), (1, ev_a, 2), (1, ev_e, -1, 1), (2, ev_c, 1, 0),
+              (7, ev_f, -1, 0), (7, ev_b, 2, 0), (10, ev_b, 2, 1), (10, ev_f, -1, 1), (11, ev_c, 1, 1),
+              (12, ev_g, -1, 0), (13, ev_e, 0, 0))
+
+    def run_events(r, base, steps, t):
+        for p in sorted({e[0] for e in events if base <= e[0] < base + steps}):
+            @pl.when(t == p - base)
+            def _():
+                for e in events:
+                    if e[0] == p:
+                        guarded(e[1], r + e[2], *e[3:])
 
     def round_(step, carry):
         r = step - 2
@@ -151,7 +169,8 @@
 
         @pl.when(valid)
         def _():
-            ag3(r % NC).wait()
+            for h in range(H):
+                ag3(r % NC, h).wait()
 
         def t1(t, carry):
             @pl.when(valid)
@@ -166,12 +185,7 @@
                 z = jnp.dot(h8[ctx], w1b[i % NB], preferred_element_type=F32)
                 abuf[:, pl.ds(pl.multiple_of(t * TN1, TN1), TN1)] = jax.nn.gelu(z).astype(BF)
 
-            @pl.when(t == 1)
-            def _():
-                guarded(ev_e, r - 1)
-                guarded(ev_g, r - 2)
-                guarded(ev_a, r + 2)
-                guarded(ev_c, r + 1)
+            run_events(r, 0, NT1, t)
             return carry
 
         lax.fori_loop(0, NT1, t1, 0)
@@ -193,9 +207,7 @@
                 def _():
                     rs0_piece(ctx, t - 1).start()
 
-            @pl.when(t == 2)
-            def _():
-                guarded(ev_b, r + 2)
+            run_events(r, NT1, NT2, t)
             return carry
 
         lax.fori_loop(0, NT2, t2, 0)
@@ -203,17 +215,18 @@
         @pl.when(valid)
         def _():
             rs0_piece(r % NC, NT2 - 1).start()
-        guarded(ev_f, r - 1)
         return carry
 
     lax.fori_loop(0, U + 4, round_, 0)
 
     def drain(k, carry):
-        ocopy(k).wait()
+        for h in range(H):
+            ocopy(k, h).wait()
 
         @pl.when(stage == 0)
         def _():
-            zcopy(k).wait_send()
+            for h in range(H):
+                zcopy(k, h).wait_send()
         return carry
 
     lax.fori_loop(0, n, drain, 0)
@@ -241,11 +254,11 @@
                 pltpu.VMEM((8 * c, F), BF),
                 pltpu.VMEM((NB, D, TN1), BF),
                 pltpu.VMEM((NB, F, TN2), BF),
-                pltpu.SemaphoreType.DMA((6, NC)),
-                pltpu.SemaphoreType.DMA((6, NC)),
-                pltpu.SemaphoreType.DMA((n,)),
-                pltpu.SemaphoreType.DMA((n,)),
-                pltpu.SemaphoreType.DMA((n,)),
+                pltpu.SemaphoreType.DMA((6 * H, NC)),
+                pltpu.SemaphoreType.DMA((6 * H, NC)),
+                pltpu.SemaphoreType.DMA((n, H)),
+                pltpu.SemaphoreType.DMA((n, H)),
+                pltpu.SemaphoreType.DMA((n, H)),
                 pltpu.SemaphoreType.DMA,
                 pltpu.SemaphoreType.DMA((NB,)),
                 pltpu.SemaphoreType.DMA((NB,)),

time: 805 us -> 707 us (0.88)
  Pallas kernels: 798 us -> 701 us
    pallas_call x1, Pallas kernels: 798 us -> 701 us  [local(): pl.pallas_call(_kernel, out_shape=jax.ShapeDtypeStruct((n, c, D), BF), in...]
where the time goes in v2:
time: 707 us
  Pallas kernels  701 us (99%)
    pallas_call x1, Pallas kernels, local(): pl.pallas_call(_kernel, out_shape=jax.ShapeDtypeStruct((n, c, D), BF), in...  701 us

profile of v2, /device:TPU:8, one launch (start us, length us, event | category | flops | bytes accessed | tf_op | source)
XLA Modules:
  0.0 707.2 jit_solution(15824422212028692934)
XLA Ops:
  0.0 1.4 copy.5.g_ref
  1.4 701.2 %shard_map.46 = bf16[16,32,4096]{2,1,0:T(8,128)(2,1)} custom-call(bf16[16,32,4096]{2,1,0:T(8,128)(2,1)} %bitcast.8, bf16[2,1,4096]{2,1,0:T(2,128)(2,1)} %copy.5.g_ref, bf16[2,4096,1792]{2,1,0:T(8,128)(2,1)} %bitcast.5, bf16[2,1792,4096]{2,1,0:T(8,128)(2,1)} %bitcast.6), custom_call_target="tpu_custom_call" | custom-call | tf_op jit(solution)/shard_map/pallas_call | solution.py:242
  702.5 4.7 copy.7

commit v3 on v2

--- a/solution.py
+++ b/solution.py
@@ -66,6 +66,9 @@
         cols = pl.ds(h * DH, DH)
         return pltpu.make_async_copy(ybuf.at[k, :, cols], out_ref.at[k, :, cols], osem.at[k, h])
 
+    def xcopy(k):
+        return pltpu.make_async_copy(x_ref.at[k], ybuf.at[k], xsem.at[k])
+
     def w1copy(i):
         cols = pl.ds(pl.multiple_of((i % NT1) * TN1, TN1), TN1)
         return pltpu.make_async_copy(w1_ref.at[(i // (NT1 * NC)) % nb, :, cols], w1b.at[i % NB], w1s.at[i % NB])
@@ -74,19 +77,17 @@
         cols = pl.ds(pl.multiple_of((i % NT2) * TN2, TN2), TN2)
         return pltpu.make_async_copy(w2_ref.at[(i // (NT2 * NC)) % nb, :, cols], w2b.at[i % NB], w2s.at[i % NB])
 
+    barrier = pltpu.get_barrier_semaphore()
+    for to in ((stage, p1), (stage, p2), (stage, sib), (1 - stage, tp)):
+        pl.semaphore_signal(barrier, inc=1, device_id=to, device_id_type=MESH)
+
+    @pl.when(stage == 0)
+    def _():
+        for k in range(n):
+            xcopy(k).start()
     for i in range(NB - 1):
         w1copy(i).start()
         w2copy(i).start()
-
-    @pl.when(stage == 0)
-    def _():
-        cp = pltpu.make_async_copy(x_ref, ybuf, xsem)
-        cp.start()
-        cp.wait()
-
-    barrier = pltpu.get_barrier_semaphore()
-    for to in ((stage, p1), (stage, p2), (stage, sib), (1 - stage, tp)):
-        pl.semaphore_signal(barrier, inc=1, device_id=to, device_id_type=MESH)
     pl.semaphore_wait(barrier, 4)
 
     def ev_a(u):
@@ -96,11 +97,18 @@
         def _():
             for h in range(H):
                 zcopy(k, h).wait_recv()
+
+        @pl.when(jnp.logical_and(stage == 0, b == 0))
+        def _():
+            xcopy(k).wait()
         yf = ybuf[k].astype(F32)
         mu = jnp.mean(yf, axis=-1, keepdims=True)
         yc = yf - mu
         var = jnp.mean(jnp.square(yc), axis=-1, keepdims=True)
-        gb = g_ref[b].astype(F32)
+        ga = g_ref[...].astype(F32)
+        gb = ga[0:1]
+        for i in range(1, nb):
+            gb = jnp.where(b == i, ga[i:i + 1], gb)
         h8[ctx, pl.ds(0, c), :] = (yc * lax.rsqrt(var + EPS) * gb).astype(BF)
         for h in range(H):
             ag1(ctx, h).start()
@@ -151,17 +159,20 @@
         def _():
             f(u, *h)
 
-    events = ((1, ev_g, -2, 1), (1, ev_a, 2), (1, ev_e, -1, 1), (2, ev_c, 1, 0),
-              (7, ev_f, -1, 0), (7, ev_b, 2, 0), (10, ev_b, 2, 1), (10, ev_f, -1, 1), (11, ev_c, 1, 1),
-              (12, ev_g, -1, 0), (13, ev_e, 0, 0))
+    tables = (
+        ((1, ev_e, -1, 1), (5, ev_b, 1, 1), (6, ev_c, 1, 0), (6, ev_f, -1, 0), (8, ev_f, -1, 1), (9, ev_a, 2),
+         (12, ev_g, -1, 0), (12, ev_e, 0, 0), (13, ev_c, 1, 1), (13, ev_g, -1, 1), (14, ev_b, 2, 0)),
+        ((0, ev_g, -3, 1), (0, ev_a, 1), (2, ev_f, -2, 1), (5, ev_b, 1, 0), (5, ev_b, 1, 1), (6, ev_e, -1, 1),
+         (7, ev_g, -2, 0), (10, ev_f, -1, 0), (11, ev_c, 1, 0), (12, ev_e, 0, 0), (13, ev_c, 1, 1)))
 
     def run_events(r, base, steps, t):
-        for p in sorted({e[0] for e in events if base <= e[0] < base + steps}):
-            @pl.when(t == p - base)
-            def _():
-                for e in events:
-                    if e[0] == p:
-                        guarded(e[1], r + e[2], *e[3:])
+        for st, events in enumerate(tables):
+            for p in sorted({e[0] for e in events if base <= e[0] < base + steps}):
+                @pl.when(jnp.logical_and(stage == st, t == p - base))
+                def _():
+                    for e in events:
+                        if e[0] == p:
+                            guarded(e[1], r + e[2], *e[3:])
 
     def round_(step, carry):
         r = step - 2
@@ -217,7 +228,7 @@
             rs0_piece(r % NC, NT2 - 1).start()
         return carry
 
-    lax.fori_loop(0, U + 4, round_, 0)
+    lax.fori_loop(0, U + 5, round_, 0)
 
     def drain(k, carry):
         for h in range(H):
@@ -259,13 +270,13 @@
                 pltpu.SemaphoreType.DMA((n, H)),
                 pltpu.SemaphoreType.DMA((n, H)),
                 pltpu.SemaphoreType.DMA((n, H)),
-                pltpu.SemaphoreType.DMA,
+                pltpu.SemaphoreType.DMA((n,)),
                 pltpu.SemaphoreType.DMA((NB,)),
                 pltpu.SemaphoreType.DMA((NB,)),
             ],
             compiler_params=pltpu.CompilerParams(
                 collective_id=0, has_side_effects=True, vmem_limit_bytes=60 * 1024 * 1024),
-        )(x.reshape(n, c, D), g[0][:, None], w1[0], w2[0])
+        )(x.reshape(n, c, D), g[0], w1[0], w2[0])
         return out.reshape(1, M, T, D)
 
     return jax.shard_map(

time: 707 us -> 691 us (0.977)
  Pallas kernels: 701 us -> 686 us
    pallas_call x1, Pallas kernels: 701 us -> 686 us  [local(): pl.pallas_call(_kernel, out_shape=jax.ShapeDtypeStruct((n, c, D), BF), in...]
where the time goes in v3:
time: 691 us
  Pallas kernels  686 us (99%)
    pallas_call x1, Pallas kernels, local(): pl.pallas_call(_kernel, out_shape=jax.ShapeDtypeStruct((n, c, D), BF), in...  686 us

profile of v3, /device:TPU:8, one launch (start us, length us, event | category | flops | bytes accessed | tf_op | source)
XLA Modules:
  0.0 690.6 jit_solution(16993369137245628281)
XLA Ops:
  0.0 685.9 %shard_map.46 = bf16[16,32,4096]{2,1,0:T(8,128)(2,1)} custom-call(bf16[16,32,4096]{2,1,0:T(8,128)(2,1)} %bitcast.8, bf16[2,4096]{1,0:T(2,128)(2,1)} %bitcast.9, bf16[2,4096,1792]{2,1,0:T(8,128)(2,1)} %bitcast.5, bf16[2,1792,4096]{2,1,0:T(8,128)(2,1)} %bitcast.6), custom_call_target="tpu_custom_call" | custom-call | tf_op jit(solution)/shard_map/pallas_call | solution.py:253
  685.9 4.7 copy.6

commit v4 on v3

--- a/solution.py
+++ b/solution.py
@@ -17,10 +17,11 @@
 TN1, TN2 = 256, 512
 NB = 4
 H = 2
+LENT = 2
 
 
 def _kernel(x_ref, g_ref, w1_ref, w2_ref, out_ref, ybuf, h8, p8, r0, r1, r2, abuf, w1b, w2b,
-            ssem, rsem, zs, zr, osem, xsem, w1s, w2s):
+            ssem, rsem, zs, zr, osem, xsem, w1s, w2s, hz, gz, hs, hr, hx):
     n, c, D = x_ref.shape
     nb, _, F = w1_ref.shape
     NT1, NT2 = F // TN1, D // TN2
@@ -69,6 +70,32 @@
     def xcopy(k):
         return pltpu.make_async_copy(x_ref.at[k], ybuf.at[k], xsem.at[k])
 
+    def lent(u):
+        return jnp.logical_and(stage == 0, jnp.logical_and(u >= LENT, u < NC))
+
+    def hcopy(j, i, h):
+        src, dst, to = (
+            (part(hz, i, 0, 1, h), part(hz, i, 1, 2, h), (stage, p1)),
+            (part(hz, i, 0, 2, h), part(hz, i, 2, 4, h), (stage, p2)),
+            (part(hz, i, 1, 4, h), part(h8, LENT + i, 1, 4, h), (1 - stage, tp)))[j]
+        return pltpu.make_async_remote_copy(
+            src_ref=src, dst_ref=dst, send_sem=hs.at[j * H + h, i], recv_sem=hr.at[j * H + h, i],
+            device_id=to, device_id_type=MESH)
+
+    def gcopy():
+        return pltpu.make_async_remote_copy(
+            src_ref=g_ref, dst_ref=gz, send_sem=hs.at[3 * H, 0], recv_sem=hr.at[3 * H, 0],
+            device_id=(1 - stage, tp), device_id_type=MESH)
+
+    def hxcopy(i):
+        return pltpu.make_async_copy(x_ref.at[LENT + i], hz.at[i, pl.ds(0, c)], hx.at[i])
+
+    def norm(y, gain):
+        yf = y.astype(F32)
+        yc = yf - jnp.mean(yf, axis=-1, keepdims=True)
+        var = jnp.mean(jnp.square(yc), axis=-1, keepdims=True)
+        return (yc * lax.rsqrt(var + EPS) * gain).astype(BF)
+
     def w1copy(i):
         cols = pl.ds(pl.multiple_of((i % NT1) * TN1, TN1), TN1)
         return pltpu.make_async_copy(w1_ref.at[(i // (NT1 * NC)) % nb, :, cols], w1b.at[i % NB], w1s.at[i % NB])
@@ -90,6 +117,29 @@
         w2copy(i).start()
     pl.semaphore_wait(barrier, 4)
 
+    @pl.when(stage == 0)
+    def _():
+        gcopy().start()
+
+    @pl.when(stage == 1)
+    def _():
+        each = [(i, h) for i in range(NC - LENT) for h in range(H)]
+        for i in range(NC - LENT):
+            hxcopy(i).start()
+        gcopy().wait_recv()
+        gain = gz[...].astype(F32)[0:1]
+        for i in range(NC - LENT):
+            hxcopy(i).wait()
+            hz[i, pl.ds(0, c), :] = norm(hz[i, pl.ds(0, c), :], gain)
+            for h in range(H):
+                hcopy(0, i, h).start()
+        for j in (0, 1):
+            for i, h in each:
+                hcopy(j, i, h).wait()
+                hcopy(j + 1, i, h).start()
+        for i, h in each:
+            hcopy(2, i, h).wait_send()
+
     def ev_a(u):
         ctx, k, b = unit(u)
 
@@ -101,26 +151,35 @@
         @pl.when(jnp.logical_and(stage == 0, b == 0))
         def _():
             xcopy(k).wait()
-        yf = ybuf[k].astype(F32)
-        mu = jnp.mean(yf, axis=-1, keepdims=True)
-        yc = yf - mu
-        var = jnp.mean(jnp.square(yc), axis=-1, keepdims=True)
         ga = g_ref[...].astype(F32)
         gb = ga[0:1]
         for i in range(1, nb):
             gb = jnp.where(b == i, ga[i:i + 1], gb)
-        h8[ctx, pl.ds(0, c), :] = (yc * lax.rsqrt(var + EPS) * gb).astype(BF)
-        for h in range(H):
-            ag1(ctx, h).start()
+        h8[ctx, pl.ds(0, c), :] = norm(ybuf[k], gb)
+
+        @pl.when(jnp.logical_not(lent(u)))
+        def _():
+            for h in range(H):
+                ag1(ctx, h).start()
 
     def ev_b(u, h):
         ctx = unit(u)[0]
-        ag1(ctx, h).wait()
-        ag2(ctx, h).start()
+
+        @pl.when(jnp.logical_not(lent(u)))
+        def _():
+            ag1(ctx, h).wait()
+            ag2(ctx, h).start()
 
     def ev_c(u, h):
         ctx = unit(u)[0]
-        ag2(ctx, h).wait()
+
+        @pl.when(jnp.logical_not(lent(u)))
+        def _():
+            ag2(ctx, h).wait()
+
+        @pl.when(lent(u))
+        def _():
+            hcopy(2, u - LENT, h).wait_recv()
         ag3(ctx, h).start()
 
     def ev_e(u, h):
@@ -241,6 +300,10 @@
         return carry
 
     lax.fori_loop(0, n, drain, 0)
+
+    @pl.when(stage == 0)
+    def _():
+        gcopy().wait_send()
 
 
 def solution(mesh):
@@ -273,9 +336,14 @@
                 pltpu.SemaphoreType.DMA((n,)),
                 pltpu.SemaphoreType.DMA((NB,)),
                 pltpu.SemaphoreType.DMA((NB,)),
+                pltpu.VMEM((NC - LENT, 4 * c, D), BF),
+                pltpu.VMEM((g.shape[1], D), BF),
+                pltpu.SemaphoreType.DMA((3 * H + 1, NC - LENT)),
+                pltpu.SemaphoreType.DMA((3 * H + 1, NC - LENT)),
+                pltpu.SemaphoreType.DMA((NC - LENT,)),
             ],
             compiler_params=pltpu.CompilerParams(
-                collective_id=0, has_side_effects=True, vmem_limit_bytes=60 * 1024 * 1024),
+                collective_id=0, has_side_effects=True, vmem_limit_bytes=49 * 1024 * 1024),
         )(x.reshape(n, c, D), g[0], w1[0], w2[0])
         return out.reshape(1, M, T, D)
 

time: 691 us -> 682 us (0.987)
  Pallas kernels: 686 us -> 678 us
    pallas_call x1, Pallas kernels: 686 us -> 678 us  [local(): pl.pallas_call(_kernel, out_shape=jax.ShapeDtypeStruct((n, c, D), BF), in...]
where the time goes in v4:
time: 682 us; the launch traced here: 681 us
  Pallas kernels  678 us (99%)
    pallas_call x1, Pallas kernels, local(): pl.pallas_call(_kernel, out_shape=jax.ShapeDtypeStruct((n, c, D), BF), in...  678 us

profile of v4, /device:TPU:8, one launch (start us, length us, event | category | flops | bytes accessed | tf_op | source)
XLA Modules:
  0.0 680.8 jit_solution(9960831677163585940)
XLA Ops:
  0.0 0.0 copy-start
  0.0 0.7 copy-done
  0.7 678.1 %shard_map.46 = bf16[16,32,4096]{2,1,0:T(8,128)(2,1)S(1)} custom-call(bf16[16,32,4096]{2,1,0:T(8,128)(2,1)} %bitcast.9, bf16[2,4096]{1,0:T(2,128)(2,1)S(1)} %bitcast.6, bf16[2,4096,1792]{2,1,0:T(8,128)(2,1)} %bitcast.7, bf16[2,1792,4096]{2,1,0:T(8,128)(2,1)} %bitcast.8), custom_call_target="tpu_custom_call" | custom-call | tf_op jit(solution)/shard_map/pallas_call | solution.py:316
  678.8 2.0 copy.6
Async XLA Ops:
  0.0 0.7 copy-start
